TPU v7x, 256 devices: a whole 4x4x8 slice. The times are simulated.
256 devices in a mesh: unit: 4 (over x), replica: 16 (over z, core), model: 4 (over y).
Axes of the slice: x: 4, y: 4, z: 8, core: 2. Of those that a mesh axis runs over, the one named last changes fastest.
Arguments:
- slope_up: float32 [64, 768, 3072], P(('unit', 'replica'), None, 'model'), parts along dimension 0, may hold values from -0.875 to 0.875
- slope_down: float32 [64, 3072, 768], P(('unit', 'replica'), 'model'), parts along dimension 0, may hold values from -0.875 to 0.875
- slope_query: float32 [64, 768, 768], P(('unit', 'replica'), None, 'model'), parts along dimension 0, may hold values from -0.875 to 0.875
- slope_key: float32 [64, 768, 768], P(('unit', 'replica'), None, 'model'), parts along dimension 0, may hold values from -0.875 to 0.875
- slope_value: float32 [64, 768, 768], P(('unit', 'replica'), None, 'model'), parts along dimension 0, may hold values from -0.875 to 0.875
- slope_mixed: float32 [64, 768, 768], P(('unit', 'replica'), 'model'), parts along dimension 0, may hold values from -0.875 to 0.875
- slope_norm: float32 [64, 768], P(('unit', 'replica')), parts along dimension 0, may hold values from -8 to 8
- param_up: float32 [3072, 3072], P(('unit', 'replica'), 'model'), parts along dimension 0, may hold values from -0.21875 to 0.21875
- param_down: float32 [12288, 768], P(('unit', 'model'), 'replica'), parts along dimension 0, may hold values from -0.109375 to 0.109375
- param_query: float32 [3072, 768], P(('unit', 'replica'), 'model'), parts along dimension 0, may hold values from -0.21875 to 0.21875
- param_key: float32 [3072, 768], P(('unit', 'replica'), 'model'), parts along dimension 0, may hold values from -0.21875 to 0.21875
- param_value: float32 [3072, 768], P(('unit', 'replica'), 'model'), parts along dimension 0, may hold values from -0.21875 to 0.21875
- param_mixed: float32 [3072, 768], P(('unit', 'model'), 'replica'), parts along dimension 0, may hold values from -0.21875 to 0.21875
- param_norm: float32 [3072], P(('unit', 'replica')), parts along dimension 0, may hold values from 0.25 to 1.75
Outputs:
- half_up: bfloat16 [3072, 3072], P('unit', 'model'), parts along dimension 0
- half_down: bfloat16 [12288, 768], P(('unit', 'model')), parts along dimension 0
- half_query: bfloat16 [3072, 768], P('unit', 'model'), parts along dimension 0
- half_key: bfloat16 [3072, 768], P('unit', 'model'), parts along dimension 0
- half_value: bfloat16 [3072, 768], P('unit', 'model'), parts along dimension 0
- half_mixed: bfloat16 [3072, 768], P(('unit', 'model')), parts along dimension 0
- half_norm: bfloat16 [3072], P('unit'), parts along dimension 0
- next_up: float32 [3072, 3072], P(('unit', 'replica'), 'model'), parts along dimension 0
- next_down: float32 [12288, 768], P(('unit', 'model'), 'replica'), parts along dimension 0
- next_query: float32 [3072, 768], P(('unit', 'replica'), 'model'), parts along dimension 0
- next_key: float32 [3072, 768], P(('unit', 'replica'), 'model'), parts along dimension 0
- next_value: float32 [3072, 768], P(('unit', 'replica'), 'model'), parts along dimension 0
- next_mixed: float32 [3072, 768], P(('unit', 'model'), 'replica'), parts along dimension 0
- next_norm: float32 [3072], P(('unit', 'replica')), parts along dimension 0
There are 4 independent parts, one for each index of `unit`. A program takes and returns all parts, laid end to end along the dimension named above; each array names one. Nothing has to cross between parts.
All inputs are finite; a program needn't handle non-finite values.
Results may differ from a plain program's by a relative error of at most 0.001.
Values may be sent and summed in bfloat16 or wider, within the bound.
No kernel may reach another device: no remote copies, remote signals or barrier semaphores. Data moves between devices by JAX's collectives and lax.ppermute only.
A program may use at most 64 MiB of HBM per device.

v0:
```python
import jax
import jax.numpy as jnp
from jax import lax
from jax.sharding import PartitionSpec as P

learn_rate = 0.3


def split_up(array, dim, size):
    lengths = array.shape
    parts = array.reshape(*lengths[:dim], size, lengths[dim] // size, *lengths[dim + 1 :])
    return jnp.moveaxis(parts, dim, 0)


def sum_together(arrays, axis, dims):
    size = lax.axis_size(axis)
    parts = [split_up(a, dim, size) for a, dim in zip(arrays, dims)]
    lines = jnp.concatenate([b.reshape(size, -1) for b in parts], axis=1)
    width = max(16, -(-lines.shape[1] // 1024) * 8)
    lines = jnp.pad(lines, ((0, 0), (0, width * 128 - lines.shape[1]))).reshape(-1, 128)
    vector, at, finished = (lax.psum_scatter(lines, axis, tiled=True).reshape(-1), 0, [])
    for b in parts:
        part = b[0]
        finished.append(vector[at : at + part.size].reshape(part.shape))
        at += part.size
    return tuple(finished)


def rows_first(arrays, axis, dims):
    turned = [jnp.moveaxis(a, dim, 0) for a, dim in zip(arrays, dims)]
    both = jnp.concatenate([t.reshape(len(t), -1) for t in turned], axis=1)
    out, at, finished = (lax.all_gather(both, axis, axis=0, tiled=True), 0, [])
    for t, dim in zip(turned, dims):
        slab = out[:, at : at + t[0].size].reshape(-1, *t.shape[1:])
        finished.append(jnp.moveaxis(slab, 0, dim))
        at += t[0].size
    return tuple(finished)


def shards(
    slope_up,
    slope_down,
    slope_query,
    slope_key,
    slope_value,
    slope_mixed,
    slope_norm,
    param_up,
    param_down,
    param_query,
    param_key,
    param_value,
    param_mixed,
    param_norm,
):
    mean_up, mean_down, mean_query, mean_key, mean_value, mean_mixed, mean_norm = sum_together(
        (
            slope_up[0],
            slope_down[0],
            slope_query[0],
            slope_key[0],
            slope_value[0],
            slope_mixed[0],
            slope_norm[0],
        ),
        "replica",
        (0, 1, 0, 0, 0, 1, 0),
    )
    mean_rate = lax.axis_size("replica") ** (-0.5)
    mean_up = mean_up * mean_rate
    mean_down = mean_down * mean_rate
    mean_query = mean_query * mean_rate
    mean_key = mean_key * mean_rate
    mean_value = mean_value * mean_rate
    mean_mixed = mean_mixed * mean_rate
    mean_norm = mean_norm * mean_rate
    next_up = param_up - learn_rate * mean_up
    next_down = param_down - learn_rate * mean_down
    next_query = param_query - learn_rate * mean_query
    next_key = param_key - learn_rate * mean_key
    next_value = param_value - learn_rate * mean_value
    next_mixed = param_mixed - learn_rate * mean_mixed
    next_norm = param_norm - learn_rate * mean_norm
    half_up, half_down, half_query, half_key, half_value, half_mixed, half_norm = rows_first(
        (
            next_up.astype(jnp.bfloat16),
            next_down.astype(jnp.bfloat16),
            next_query.astype(jnp.bfloat16),
            next_key.astype(jnp.bfloat16),
            next_value.astype(jnp.bfloat16),
            next_mixed.astype(jnp.bfloat16),
            next_norm.astype(jnp.bfloat16),
        ),
        "replica",
        (0, 1, 0, 0, 0, 1, 0),
    )
    return (
        half_up,
        half_down,
        half_query,
        half_key,
        half_value,
        half_mixed,
        half_norm,
        next_up,
        next_down,
        next_query,
        next_key,
        next_value,
        next_mixed,
        next_norm,
    )


def solution(mesh):
    placed = (
        P(("unit", "replica"), None, "model"),
        P(("unit", "replica"), "model", None),
        P(("unit", "replica"), None, "model"),
        P(("unit", "replica"), None, "model"),
        P(("unit", "replica"), None, "model"),
        P(("unit", "replica"), "model", None),
        P(("unit", "replica"), None),
        P(("unit", "replica"), "model"),
        P(("unit", "model"), "replica"),
        P(("unit", "replica"), "model"),
        P(("unit", "replica"), "model"),
        P(("unit", "replica"), "model"),
        P(("unit", "model"), "replica"),
        P(("unit", "replica")),
    )
    return jax.shard_map(
        shards,
        mesh=mesh,
        in_specs=placed,
        out_specs=(
            P("unit", "model"),
            P(("unit", "model"), None),
            P("unit", "model"),
            P("unit", "model"),
            P("unit", "model"),
            P(("unit", "model"), None),
            P("unit"),
            P(("unit", "replica"), "model"),
            P(("unit", "model"), "replica"),
            P(("unit", "replica"), "model"),
            P(("unit", "replica"), "model"),
            P(("unit", "replica"), "model"),
            P(("unit", "model"), "replica"),
            P(("unit", "replica")),
        ),
        check_vma=False,
    )
```

profile of v0, /device:TPU:1, one launch (start us, length us, event | category | flops | bytes accessed | tf_op | source)
XLA Modules:
  0.0 258.9 jit_solution(8501076146839965189)
XLA Ops:
  7.2 1.9 reshape_reshape_squeeze.12
  9.1 1.6 constant_dynamic-update-slice_fusion.6
  10.7 2.0 copy.69
  12.7 4.1 %copy.70 = f32[16,768,48]{2,1,0:T(8,128)} copy(f32[16,768,48]{1,2,0:T(8,128)S(1)} %bitcast.19) | data formatting | bytes 4718592 | tf_op jit(solution)/shard_map/transpose | solution.py:12
  16.8 7.3 %reshape.76 = f32[16,36864]{1,0:T(8,128)S(1)} reshape(f32[16,768,48]{2,1,0:T(8,128)} %copy.70) | data formatting | bytes 4718592 | tf_op jit(solution)/shard_map/reshape | solution.py:18
  24.1 1.3 copy.71
  25.5 1.1 reshape_reshape_squeeze.13
  26.6 1.3 copy.72
  27.9 1.1 reshape_reshape_squeeze.14
  29.0 1.3 copy.73
  30.4 1.1 reshape_reshape_squeeze.15
  31.5 1.3 copy.74
  32.8 1.7 copy.75
  34.5 3.5 %reshape.77 = f32[16,9216]{1,0:T(8,128)} reshape(f32[16,192,48]{2,1,0:T(8,128)} %copy.75) | data formatting | bytes 1179648 | tf_op jit(solution)/shard_map/reshape | solution.py:18
  38.1 1.6 constant_dynamic-update-slice_fusion.5
  39.7 0.9 constant_dynamic-update-slice_fusion.4
  40.6 0.9 constant_dynamic-update-slice_fusion.3
  41.4 0.9 constant_dynamic-update-slice_fusion.2
  42.3 0.9 constant_dynamic-update-slice_fusion.1
  43.2 0.6 constant_dynamic-update-slice_fusion
  43.8 6.4 %pad.4 = f32[16,111616]{1,0:T(8,128)} pad(f32[16,110640]{1,0:T(8,128)} %constant_dynamic-update-slice_fusion, f32[]{:T(128)} %constant.8.clone.1), padding=0_0x0_976 | pad | bytes 14224388 | tf_op jit(solution)/shard_map/jit(_pad)/pad | solution.py:20
  50.1 5.5 %reshape.78 = f32[13952,128]{1,0:T(8,128)} reshape(f32[16,111616]{1,0:T(8,128)} %pad.4) | data formatting | bytes 14286848 | tf_op jit(solution)/shard_map/reshape | solution.py:20
  55.8 0.5 copy-done.12
  56.3 0.6 dynamic-slice
  57.5 132.0 %all-reduce.4.cloned.1.call-done = f32[13952,128]{1,0:T(8,128)} async-done(((f32[13952,128]{1,0:T(8,128)}), f32[13952,128]{1,0:T(8,128)}) %all-reduce.4.cloned.1.call-update) | async-done | bytes 7143440
  189.5 1.0 dynamic-slice_multiply_fusion
  190.6 0.2 mul.64
  190.7 0.1 copy.76
  190.9 0.9 dynamic-slice_multiply_fusion.2
  192.0 0.1 mul.73
  192.2 1.1 dynamic-slice_bitcast_fusion
  193.3 0.5 convert_bitcast_fusion.2
  193.8 0.1 copy.78
  193.9 0.7 fusion.5
  194.6 0.7 convert_bitcast_fusion
  195.2 0.6 fusion.4
  195.9 0.6 convert_bitcast_fusion.1
  196.5 0.6 fusion.2
  197.2 0.8 concatenate.7
  198.0 42.8 %all-gather.2.cloned.1.call-done = bf16[768,2305]{1,0:T(8,128)(2,1)} async-done(((bf16[48,2305]{1,0:T(8,128)(2,1)}), bf16[768,2305]{1,0:T(8,128)(2,1)}) %all-gather.2.cloned.1.call-update) | async-done | bytes 3540496 | tf_op jit(solution)/shard_map/all_gather | solution.py:32
  240.8 2.8 %slice_bitcast_fusion = (bf16[768,768]{0,1:T(8,128)(2,1)S(1)}, bf16[768,768]{1,0:T(8,128)(2,1)}) fusion(bf16[768,2305]{1,0:T(8,128)(2,1)} %all-gather.2.cloned.1.call-done), kind=kLoop, calls=%fused_computation | loop fusion | bytes 4718592 | tf_op jit(solution)/shard_map/transpose | solution.py:35
  243.6 1.4 copy.79
  245.0 1.9 slice_bitcast_fusion.1
  246.9 0.9 copy.80
  247.8 0.9 copy.81
  248.7 0.9 copy.82
  249.5 0.9 copy.83
  250.4 1.7 slice_reduce_fusion
  (36 shorter events, 0.6 us)
Async XLA Ops:
  7.2 182.3 %all-reduce.4.cloned.1.call-start = ((), (), s32[]{:S(2)}) async-start(), calls=%async_computation.1 | async-start | bytes 14286848
  24.1 13.9 %copy-start.10 = (f32[1,768]{1,0:T(1,128)S(1)}, f32[1,768]{1,0:T(1,128)}, u32[]{:S(2)}) copy-start(f32[1,768]{1,0:T(1,128)} %param.20) | copy-start | bytes 9220
  34.5 5.1 %copy-start = (f32[16,9216]{1,0:T(8,128)S(1)}, f32[16,9216]{1,0:T(8,128)}, u32[]{:S(2)}) copy-start(f32[16,9216]{1,0:T(8,128)} %reshape_reshape_squeeze.13) | copy-start | bytes 1769476
  34.5 6.0 %copy-start.1 = (f32[16,9216]{1,0:T(8,128)S(1)}, f32[16,9216]{1,0:T(8,128)}, u32[]{:S(2)}) copy-start(f32[16,9216]{1,0:T(8,128)} %reshape_reshape_squeeze.14) | copy-start | bytes 1769476
  38.1 3.3 %copy-start.2 = (f32[16,9216]{1,0:T(8,128)S(1)}, f32[16,9216]{1,0:T(8,128)}, u32[]{:S(2)}) copy-start(f32[16,9216]{1,0:T(8,128)} %reshape_reshape_squeeze.15) | copy-start | bytes 1769476
  38.1 4.2 %copy-start.3 = (f32[16,9216]{1,0:T(8,128)S(1)}, f32[16,9216]{1,0:T(8,128)}, u32[]{:S(2)}) copy-start(f32[16,9216]{1,0:T(8,128)} %reshape.77) | copy-start | bytes 1769476
  55.6 0.7 copy-start.12
  55.6 137.6 %copy-start.11 = (f32[48]{0:T(128)S(1)}, f32[48]{0:T(128)}, u32[]{:S(2)}) copy-start(f32[48]{0:T(128)} %param.27) | copy-start | bytes 580
  55.6 138.3 %copy-start.4 = (f32[48,768]{1,0:T(8,128)S(1)}, f32[48,768]{1,0:T(8,128)}, u32[]{:S(2)}) copy-start(f32[48,768]{1,0:T(8,128)} %param.21) | copy-start | bytes 442372
  55.6 138.9 %copy-start.5 = (f32[768,48]{0,1:T(8,128)S(1)}, f32[768,48]{0,1:T(8,128)}, u32[]{:S(2)}) copy-start(f32[768,48]{0,1:T(8,128)} %param.22) | copy-start | bytes 442372
  55.6 139.6 %copy-start.6 = (f32[48,192]{1,0:T(8,128)S(1)}, f32[48,192]{1,0:T(8,128)}, u32[]{:S(2)}) copy-start(f32[48,192]{1,0:T(8,128)} %param.23) | copy-start | bytes 110596
  55.6 140.2 %copy-start.7 = (f32[192,48]{0,1:T(8,128)S(1)}, f32[192,48]{0,1:T(8,128)}, u32[]{:S(2)}) copy-start(f32[192,48]{0,1:T(8,128)} %param.26) | copy-start | bytes 110596
  55.7 140.8 %copy-start.8 = (f32[48,192]{1,0:T(8,128)S(1)}, f32[48,192]{1,0:T(8,128)}, u32[]{:S(2)}) copy-start(f32[48,192]{1,0:T(8,128)} %param.25) | copy-start | bytes 110596
  55.7 140.8 %copy-start.9 = (f32[48,192]{1,0:T(8,128)S(1)}, f32[48,192]{1,0:T(8,128)}, u32[]{:S(2)}) copy-start(f32[48,192]{1,0:T(8,128)} %param.24) | copy-start | bytes 110596
  55.7 185.1 %all-gather.2.cloned.1.call-start = ((), (), s32[]{:S(2)}) async-start(), calls=%async_computation | async-start | bytes 3969024 | tf_op jit(solution)/shard_map/all_gather | solution.py:32
Sparse Core Ops, SparseCore 0:
  55.8 133.6 all-reduce.3
  198.1 42.6 all-gather.1
where the time goes:
time: 259 us
  waiting for transfers between devices  175 us (68%)
  local copies, waits for them, and re-layouts  63.4 us (24%)
  between operations  14.9 us (6%)
  other arithmetic  5.71 us (2%)
    unnamed x3, waiting for transfers between devices  132 us
    all_gather x1, waiting for transfers between devices, rows_first(): out, at, finished = (lax.all_gather(both, axis, axis=0, tiled=True), 0, [])  42.8 us
    unnamed x43, local copies, waits for them, and re-layouts  20.1 us
    reshape x2, local copies, waits for them, and re-layouts, sum_together(): lines = jnp.concatenate([b.reshape(size, -1) for b in parts], axis=1)  10.8 us
    pad x1, local copies, waits for them, and re-layouts, sum_together(): jnp.pad(lines, ((0, 0), (0, width * 128 - lines.shape[1]))).reshape(-1, 128)  6.35 us
    transpose x2, local copies, waits for them, and re-layouts, split_up(): return jnp.moveaxis(parts, dim, 0)  5.77 us
    reshape x1, local copies, waits for them, and re-layouts, sum_together(): jnp.pad(lines, ((0, 0), (0, width * 128 - lines.shape[1]))).reshape(-1, 128)  5.49 us
    another operation x4, local copies, waits for them, and re-layouts, sum_together(): lines = jnp.concatenate([b.reshape(size, -1) for b in parts], axis=1)  5.22 us
  transfers between devices with their start and end apart: 2, of which 2 were waited for; matrix products, arithmetic and copies ran while one was open for 0% of the time, Pallas kernels for 0%

commit v1 on v0

--- a/solution.py
+++ b/solution.py
@@ -29,7 +29,13 @@
 def rows_first(arrays, axis, dims):
     turned = [jnp.moveaxis(a, dim, 0) for a, dim in zip(arrays, dims)]
     both = jnp.concatenate([t.reshape(len(t), -1) for t in turned], axis=1)
-    out, at, finished = (lax.all_gather(both, axis, axis=0, tiled=True), 0, [])
+    out, at, finished = (
+        jnp.concatenate(
+            lax.all_to_all(jnp.stack([both] * lax.axis_size(axis)), axis, 0, 0), axis=0
+        ),
+        0,
+        [],
+    )
     for t, dim in zip(turned, dims):
         slab = out[:, at : at + t[0].size].reshape(-1, *t.shape[1:])
         finished.append(jnp.moveaxis(slab, 0, dim))

time: 259 us -> 305 us (1.18)
  blocking collectives: 0 us -> 93.4 us
  waiting for transfers between devices: 175 us -> 132 us
  local copies, waits for them, and re-layouts: 63.4 us -> 58.9 us
    all_to_all x0 -> x1, blocking collectives: none -> 93.4 us  [rows_first(): lax.all_to_all(jnp.stack([both] * lax.axis_size(axis)), axis, 0, 0)]
    all_gather x1 -> x0, waiting for transfers between devices: 42.8 us -> none  [rows_first(): out, at, finished = (lax.all_gather(both, axis, axis=0, tiled=True), 0, [])]
    transpose x2, local copies, waits for them, and re-layouts: 4.68 us -> 1.55 us  [rows_first(): finished.append(jnp.moveaxis(slab, 0, dim))]
    unnamed x3 -> x2, waiting for transfers between devices: 132 us -> 132 us
  transfers between devices with their start and end apart: 2 -> 1, of which waited for: 2 -> 1; matrix products, arithmetic and copies ran while one was open for 0% -> 0% of each run, Pallas kernels for 0% -> 0%
where the time goes in v1:
time: 305 us
  waiting for transfers between devices  132 us (43%)
  blocking collectives  93.4 us (31%)
  local copies, waits for them, and re-layouts  58.9 us (19%)
  between operations  14.9 us (5%)
  other arithmetic  5.71 us (2%)
    unnamed x2, waiting for transfers between devices  132 us
    all_to_all x1, blocking collectives, rows_first(): lax.all_to_all(jnp.stack([both] * lax.axis_size(axis)), axis, 0, 0)  93.4 us
    unnamed x43, local copies, waits for them, and re-layouts  20.1 us
    reshape x2, local copies, waits for them, and re-layouts, sum_together(): lines = jnp.concatenate([b.reshape(size, -1) for b in parts], axis=1)  10.8 us
    pad x1, local copies, waits for them, and re-layouts, sum_together(): jnp.pad(lines, ((0, 0), (0, width * 128 - lines.shape[1]))).reshape(-1, 128)  6.35 us
  transfers between devices with their start and end apart: 1, of which 1 were waited for; matrix products, arithmetic and copies ran while one was open for 0% of the time, Pallas kernels for 0%

profile of v1, /device:TPU:1, one launch (start us, length us, event | category | flops | bytes accessed | tf_op | source)
XLA Modules:
  0.0 304.8 jit_solution(17772197035838127383)
XLA Ops:
  7.2 1.9 reshape_reshape_squeeze.12
  9.1 1.5 constant_dynamic-update-slice_fusion.6
  10.6 2.0 copy.71
  12.7 4.1 %copy.72 = f32[16,768,48]{2,1,0:T(8,128)} copy(f32[16,768,48]{1,2,0:T(8,128)S(1)} %bitcast.23) | data formatting | bytes 4718592 | tf_op jit(solution)/shard_map/transpose | solution.py:12
  16.7 7.3 %reshape.81 = f32[16,36864]{1,0:T(8,128)S(1)} reshape(f32[16,768,48]{2,1,0:T(8,128)} %copy.72) | data formatting | bytes 4718592 | tf_op jit(solution)/shard_map/reshape | solution.py:18
  24.1 1.3 copy.73
  25.4 1.1 reshape_reshape_squeeze.13
  26.6 1.3 copy.74
  27.9 1.1 reshape_reshape_squeeze.14
  29.0 1.3 copy.75
  30.3 1.1 reshape_reshape_squeeze.15
  31.5 1.3 copy.76
  32.8 1.7 copy.77
  34.5 3.5 %reshape.82 = f32[16,9216]{1,0:T(8,128)} reshape(f32[16,192,48]{2,1,0:T(8,128)} %copy.77) | data formatting | bytes 1179648 | tf_op jit(solution)/shard_map/reshape | solution.py:18
  38.1 1.6 constant_dynamic-update-slice_fusion.5
  39.6 0.9 constant_dynamic-update-slice_fusion.4
  40.5 0.9 constant_dynamic-update-slice_fusion.3
  41.4 0.9 constant_dynamic-update-slice_fusion.2
  42.3 0.9 constant_dynamic-update-slice_fusion.1
  43.1 0.6 constant_dynamic-update-slice_fusion
  43.7 6.4 %pad.4 = f32[16,111616]{1,0:T(8,128)} pad(f32[16,110640]{1,0:T(8,128)} %constant_dynamic-update-slice_fusion, f32[]{:T(128)} %constant.8.clone.1), padding=0_0x0_976 | pad | bytes 14224388 | tf_op jit(solution)/shard_map/jit(_pad)/pad | solution.py:20
  50.1 5.5 %reshape.83 = f32[13952,128]{1,0:T(8,128)} reshape(f32[16,111616]{1,0:T(8,128)} %pad.4) | data formatting | bytes 14286848 | tf_op jit(solution)/shard_map/reshape | solution.py:20
  55.6 0.6 copy-done.12
  56.2 0.6 dynamic-slice
  57.5 132.0 %all-reduce.4.cloned.1.call-done = f32[13952,128]{1,0:T(8,128)} async-done(((f32[13952,128]{1,0:T(8,128)}), f32[13952,128]{1,0:T(8,128)}) %all-reduce.4.cloned.1.call-update) | async-done | bytes 7143440
  189.4 1.0 dynamic-slice_multiply_fusion
  190.5 0.2 mul.64
  190.7 0.1 copy.78
  190.8 0.9 dynamic-slice_multiply_fusion.2
  192.1 1.1 dynamic-slice_bitcast_fusion
  193.2 0.5 convert_bitcast_fusion.2
  193.7 0.1 copy.80
  193.8 0.7 fusion.5
  194.5 0.7 convert_bitcast_fusion
  195.2 0.6 fusion.4
  195.8 0.6 convert_bitcast_fusion.1
  196.4 0.6 fusion.2
  197.1 0.1 concatenate.7
  197.2 0.3 stack.2
  197.4 93.4 %all_to_all.5 = bf16[16,48,2305]{2,1,0:T(8,128)(2,1)S(1)} all-to-all(bf16[16,48,2305]{2,1,0:T(8,128)(2,1)S(1)} %stack.2), channel_id=1, replica_groups=mesh['unit'=4,'replica'=16,'model'=4] {'replica'}, dimensions={0} | all-to-all | bytes 7080960 | tf_op jit(solution)/shard_map/all_to_all | solution.py:34
  290.8 1.2 slice_bitcast_fusion
  292.0 0.4 slice_bitcast_fusion.1
  292.3 0.7 slice_reduce_fusion
  293.1 1.4 copy.81
  294.5 0.9 copy.82
  295.4 0.9 copy.83
  296.3 0.9 copy.84
  297.1 0.9 copy.85
  (35 shorter events, 0.6 us)
Async XLA Ops:
  7.2 182.2 %all-reduce.4.cloned.1.call-start = ((), (), s32[]{:S(2)}) async-start(), calls=%async_computation.1 | async-start | bytes 14286848
  24.1 13.9 %copy-start.10 = (f32[1,768]{1,0:T(1,128)S(1)}, f32[1,768]{1,0:T(1,128)}, u32[]{:S(2)}) copy-start(f32[1,768]{1,0:T(1,128)} %param.20) | copy-start | bytes 9220
  34.5 5.2 %copy-start = (f32[16,9216]{1,0:T(8,128)S(1)}, f32[16,9216]{1,0:T(8,128)}, u32[]{:S(2)}) copy-start(f32[16,9216]{1,0:T(8,128)} %reshape_reshape_squeeze.13) | copy-start | bytes 1769476
  34.5 6.0 %copy-start.1 = (f32[16,9216]{1,0:T(8,128)S(1)}, f32[16,9216]{1,0:T(8,128)}, u32[]{:S(2)}) copy-start(f32[16,9216]{1,0:T(8,128)} %reshape_reshape_squeeze.14) | copy-start | bytes 1769476
  38.1 3.3 %copy-start.2 = (f32[16,9216]{1,0:T(8,128)S(1)}, f32[16,9216]{1,0:T(8,128)}, u32[]{:S(2)}) copy-start(f32[16,9216]{1,0:T(8,128)} %reshape_reshape_squeeze.15) | copy-start | bytes 1769476
  38.1 4.2 %copy-start.3 = (f32[16,9216]{1,0:T(8,128)S(1)}, f32[16,9216]{1,0:T(8,128)}, u32[]{:S(2)}) copy-start(f32[16,9216]{1,0:T(8,128)} %reshape.82) | copy-start | bytes 1769476
  55.5 0.7 copy-start.12
  55.5 137.6 %copy-start.11 = (f32[48]{0:T(128)S(1)}, f32[48]{0:T(128)}, u32[]{:S(2)}) copy-start(f32[48]{0:T(128)} %param.27) | copy-start | bytes 580
  55.5 138.3 %copy-start.4 = (f32[48,768]{1,0:T(8,128)S(1)}, f32[48,768]{1,0:T(8,128)}, u32[]{:S(2)}) copy-start(f32[48,768]{1,0:T(8,128)} %param.21) | copy-start | bytes 442372
  55.5 138.9 %copy-start.5 = (f32[768,48]{0,1:T(8,128)S(1)}, f32[768,48]{0,1:T(8,128)}, u32[]{:S(2)}) copy-start(f32[768,48]{0,1:T(8,128)} %param.22) | copy-start | bytes 442372
  55.6 139.6 %copy-start.6 = (f32[48,192]{1,0:T(8,128)S(1)}, f32[48,192]{1,0:T(8,128)}, u32[]{:S(2)}) copy-start(f32[48,192]{1,0:T(8,128)} %param.23) | copy-start | bytes 110596
  55.6 140.2 %copy-start.7 = (f32[192,48]{0,1:T(8,128)S(1)}, f32[192,48]{0,1:T(8,128)}, u32[]{:S(2)}) copy-start(f32[192,48]{0,1:T(8,128)} %param.26) | copy-start | bytes 110596
  55.6 140.8 %copy-start.8 = (f32[48,192]{1,0:T(8,128)S(1)}, f32[48,192]{1,0:T(8,128)}, u32[]{:S(2)}) copy-start(f32[48,192]{1,0:T(8,128)} %param.25) | copy-start | bytes 110596
  55.6 140.8 %copy-start.9 = (f32[48,192]{1,0:T(8,128)S(1)}, f32[48,192]{1,0:T(8,128)}, u32[]{:S(2)}) copy-start(f32[48,192]{1,0:T(8,128)} %param.24) | copy-start | bytes 110596
Sparse Core Ops, SparseCore 0:
  55.8 133.6 all-reduce.3
